TPU v7x, 512 devices: a whole 4x8x8 slice. The times are simulated.
512 devices in a mesh: pts: 32 (over y, x), cen: 16 (over z, core).
Axes of the slice: x: 4, y: 8, z: 8, core: 2. Of those that a mesh axis runs over, the one named last changes fastest.
Arguments:
- points: bfloat16 [131072, 1024], P('pts'), may hold values from -60 to 60
- fine_assign: int32 [2, 131072], P(None, 'pts'), may hold values from 0 to 2047
- fine_start: float32 [2048, 1024], P('cen'), may hold values from -3 to 3
- coarse_start: float32 [64, 1024], replicated, may hold values from -3 to 3
- coarse_assign: int32 [2048], P('cen'), may hold values from 0 to 63
Outputs:
- fine_centroids: float32 [2048, 1024], P('cen')
- coarse_centroids: float32 [64, 1024], replicated
- gaps: float32 [2, 131072], P(None, 'pts')
All inputs are finite; a program needn't handle non-finite values.
Results may differ from a plain program's by a relative error of at most 0.0028.
Values sent between devices are 32-bit elements; how exact they have to be, the bound alone decides.
A program may use at most 64 MiB of HBM per device.

v0:
```python
import math
import jax
import jax.numpy as jnp
from jax import lax
from jax.sharding import PartitionSpec as P

NC = 64
PASSES = 2
prior_weight = 4.0


def copy_for_each(x, axis):
    size = lax.axis_size(axis)
    return lax.all_to_all(jnp.broadcast_to(x[None], (size, *x.shape)), axis, 0, 0, tiled=True)


def over_copies(x, axis):
    everything = copy_for_each(x, axis)
    return jnp.sum(everything, axis=0)


def over_copies_2(x, axis):
    everything = copy_for_each(x, axis)
    return jnp.min(everything, axis=0)


def in_blocks(x, dim, size):
    before, after = (x.shape[:dim], x.shape[dim + 1 :])
    return jnp.moveaxis(x.reshape(*before, size, -1, *after), dim, 0)


def sum_at_owner(x, axis, dim):
    blocks = in_blocks(x, dim, lax.axis_size(axis))
    arrived = lax.all_to_all(blocks, axis, split_axis=0, concat_axis=0, tiled=True)
    return arrived.sum(axis=0)


def in_one(arrays, axis):
    ends = [0]
    for a in arrays:
        ends.append(ends[-1] + a.size)
    running = over_copies(jnp.concatenate([a.ravel() for a in arrays]), axis)
    return tuple((running[b:e].reshape(a.shape) for a, b, e in zip(arrays, ends, ends[1:])))


def rows_first(arrays, axis, dims):
    turned = [jnp.moveaxis(a, dim, 0) for a, dim in zip(arrays, dims)]
    widths = [t[0].size for t in turned]
    both = jnp.concatenate([t.reshape(-1, w) for t, w in zip(turned, widths)], axis=1)
    filled = lax.all_gather(both, axis, axis=0, tiled=True)
    blocks = jnp.split(filled, [sum(widths[:k]) for k in range(1, len(widths))], axis=1)
    return tuple(
        (
            jnp.moveaxis(b.reshape(-1, *t.shape[1:]), 0, dim)
            for b, t, dim in zip(blocks, turned, dims)
        )
    )


def refine(totals, counts, coarse_cols, coarse_table):
    lookup = jnp.dot(coarse_table, coarse_cols, precision=lax.Precision.HIGHEST)
    fine_next = (totals + prior_weight * lookup) / (counts + prior_weight)[:, None]
    coarse_part = lax.dot_general(
        coarse_table,
        counts[:, None] * fine_next,
        (((0,), (0,)), ((), ())),
        precision=lax.Precision.HIGHEST,
    )
    coarse_weight = jnp.sum(coarse_table * counts[:, None], axis=0)
    return (fine_next, coarse_part, coarse_weight)


def on_device(points, fine_assign, fine_start, coarse_start, coarse_assign):
    width = points.shape[1]
    local_count = fine_start.shape[0]
    offset = lax.axis_index("cen") * local_count
    columns = jnp.arange(local_count, dtype=jnp.int32)
    coarse_table = (coarse_assign[:, None] == jnp.arange(NC, dtype=jnp.int32)[None, :]).astype(
        jnp.float32
    )
    point_values = points.astype(jnp.float32)
    squares = jnp.sum(point_values * point_values, axis=1)
    fine_now = fine_start
    coarse_now = coarse_start
    gap_rows = []
    for pass_index in range(PASSES):
        member = (fine_assign[pass_index] - offset)[:, None] == columns[None, :]
        products = jnp.dot(
            points, fine_now.astype(jnp.bfloat16).T, preferred_element_type=jnp.float32
        )
        energy = jnp.sum(fine_now * fine_now, axis=1)[None, :] - 2.0 * products
        picked_local = jnp.sum(jnp.where(member, energy, 0.0), axis=1)
        nearest_local = jnp.min(energy, axis=1)
        picked = over_copies(picked_local, "cen")
        nearest = over_copies_2(nearest_local, "cen")
        gap_rows.append((picked - nearest) / math.sqrt(width))
        weights = 1.0 / (1.0 + (squares + picked) / width)
        scaled = (point_values * weights[:, None]).astype(jnp.bfloat16)
        partial_sums = lax.dot_general(
            member.astype(jnp.bfloat16),
            scaled,
            (((0,), (0,)), ((), ())),
            preferred_element_type=jnp.float32,
        )
        partial_weights = jnp.sum(jnp.where(member, weights[:, None], 0.0), axis=0)
        share_width = width // lax.axis_size("pts")
        start = lax.axis_index("pts") * share_width
        shares = sum_at_owner(partial_sums, "pts", 1)
        counts = over_copies(partial_weights, "pts")
        coarse_cols = lax.dynamic_slice_in_dim(coarse_now, start, share_width, 1)
        fine_share, coarse_part, coarse_weight = refine(shares, counts, coarse_cols, coarse_table)
        coarse_sum, coarse_count = in_one((coarse_part, coarse_weight), "cen")
        coarse_share = (coarse_sum + prior_weight * coarse_cols) / (coarse_count + prior_weight)[
            :, None
        ]
        fine_now, coarse_now = rows_first((fine_share, coarse_share), "pts", (1, 1))
    return (fine_now, coarse_now, jnp.stack(gap_rows))


def solution(mesh):
    placed = (P("pts", None), P(None, "pts"), P("cen", None), P(), P("cen"))
    return jax.shard_map(
        on_device,
        mesh=mesh,
        in_specs=placed,
        out_specs=(P("cen", None), P(), P(None, "pts")),
        check_vma=False,
    )
```

profile of v0, /device:TPU:2, one launch (start us, length us, event | category | flops | bytes accessed | tf_op | source)
XLA Modules:
  0.0 298.8 jit_solution(10869809501321211903)
XLA Ops:
  0.6 1.2 multiply_reduce_fusion.1
  1.9 0.9 slice_subtract_fusion.1
  2.7 6.5 %fusion.33 = (f32[4096]{0:T(1024)S(1)}, f32[4096]{0:T(1024)S(1)}) fusion(s32[4096]{0:T(1024)S(1)} %bitcast.44, bf16[4096,1024]{1,0:T(8,128)(2,1)} %param.5, f32[128,1024]{1,0:T(8,128)} %param.7, f32[128]{0:T(128)S(1)} %multiply_reduce_fusion.1), kind=kOutput, calls=%fused_computation.70 | convolution fusion | flops 1077010432 | bytes 8962560 | tf_op jit(solution)/shard_map/dot_general | solution.py:88
  9.4 21.4 %all_to_all.58 = f32[16,1,4096]{2,1,0:T(1,128)S(1)} all-to-all(f32[16,1,4096]{2,1,0:T(1,128)S(1)} %broadcast_in_dim.46), channel_id=1, replica_groups=mesh['pts'=32,'cen'=16] {'cen'}, dimensions={0} | all-to-all | bytes 524288 | tf_op jit(solution)/shard_map/all_to_all | solution.py:14
  30.8 0.9 broadcast_in_dim.38
  31.7 3.5 %all-to-all-start = ((f32[16,1,4096]{2,1,0:T(1,128)}), f32[16,1,4096]{2,1,0:T(1,128)S(1)}, u32[]{:S(2)}, u32[]{:S(2)}) async-start(f32[16,1,4096]{2,1,0:T(1,128)} %broadcast_in_dim.38), calls=%async_computation | async-start | bytes 524288 | tf_op jit(solution)/shard_map/all_to_all | solution.py:14
  35.2 5.1 %fusion = f32[4096]{0:T(1024)S(1)} fusion(bf16[4096,1024]{1,0:T(8,128)(2,1)} %param.5), kind=kLoop, calls=%fused_computation.3 | loop fusion | flops 12578816 | bytes 8404992 | tf_op jit(solution)/shard_map/reduce_sum | solution.py:82
  40.5 6.0 %all-to-all-done = f32[16,1,4096]{2,1,0:T(1,128)S(1)} async-done(((f32[16,1,4096]{2,1,0:T(1,128)}), f32[16,1,4096]{2,1,0:T(1,128)S(1)}, u32[]{:S(2)}, u32[]{:S(2)}) %all-to-all-start) | async-done | bytes 262176 | tf_op jit(solution)/shard_map/all_to_all | solution.py:14
  47.7 10.2 %all-to-all-start.2 = ((f32[32,1,128]{2,1,0:T(1,128)}), f32[32,1,128]{2,1,0:T(1,128)S(1)}, u32[]{:S(2)}, u32[]{:S(2)}) async-start(f32[32,1,128]{2,1,0:T(1,128)} %broadcast_in_dim.40), calls=%async_computation.2 | async-start | bytes 32768 | tf_op jit(solution)/shard_map/all_to_all | solution.py:14
  58.0 8.1 %fusion.5 = f32[128,1024]{0,1:T(8,128)} fusion(bf16[4096,1024]{1,0:T(8,128)(2,1)} %param.5, f32[4096]{0:T(1024)S(1)} %get-tuple-element.20, s32[4096]{0:T(1024)S(1)} %bitcast.46), kind=kOutput, calls=%fused_computation.7 | convolution fusion | flops 1086849024 | bytes 8945664 | tf_op jit(solution)/shard_map/dot_general | solution.py:99
  66.5 9.4 %all-to-all-start.1 = ((f32[32,128,32]{1,2,0:T(8,128)}), f32[32,128,32]{1,2,0:T(8,128)S(1)}, u32[]{:S(2)}, u32[]{:S(2)}) async-start(f32[32,128,32]{1,2,0:T(8,128)} %bitcast.3), calls=%async_computation.1 | async-start | bytes 1048576 | tf_op jit(solution)/shard_map/all_to_all | solution.py:34
  76.1 16.8 %all-to-all-done.1 = f32[32,128,32]{1,2,0:T(8,128)S(1)} async-done(((f32[32,128,32]{1,2,0:T(8,128)}), f32[32,128,32]{1,2,0:T(8,128)S(1)}, u32[]{:S(2)}, u32[]{:S(2)}) %all-to-all-start.1) | async-done | bytes 524320 | tf_op jit(solution)/shard_map/all_to_all | solution.py:34
  93.4 0.7 broadcast_in_dim.41
  94.1 3.5 %all-to-all-start.3 = ((f32[16,1,2112]{2,1,0:T(1,128)}), f32[16,1,2112]{2,1,0:T(1,128)S(1)}, u32[]{:S(2)}, u32[]{:S(2)}) async-start(f32[16,1,2112]{2,1,0:T(1,128)} %broadcast_in_dim.41), calls=%async_computation.3 | async-start | bytes 278528 | tf_op jit(solution)/shard_map/all_to_all | solution.py:14
  97.7 8.7 %all-to-all-done.3 = f32[16,1,2112]{2,1,0:T(1,128)S(1)} async-done(((f32[16,1,2112]{2,1,0:T(1,128)}), f32[16,1,2112]{2,1,0:T(1,128)S(1)}, u32[]{:S(2)}, u32[]{:S(2)}) %all-to-all-start.3) | async-done | bytes 135200 | tf_op jit(solution)/shard_map/all_to_all | solution.py:14
  106.7 48.5 %all_gather.6 = f32[1024,192]{1,0:T(8,128)S(1)} all-gather(f32[32,192]{1,0:T(8,128)S(1)} %pad_maximum_fusion), channel_id=1, replica_groups=mesh['pts'=32,'cen'=16] {'pts'}, dimensions={0}, use_global_device_ids=true | all-gather | bytes 811008 | tf_op jit(solution)/shard_map/all_gather | solution.py:50
  155.4 6.5 %fusion.11 = (f32[4096]{0:T(1024)S(1)}, f32[128,4096]{1,0:T(8,128)S(1)}) fusion(s32[4096]{0:T(1024)S(1)} %bitcast.35, bf16[4096,1024]{1,0:T(8,128)(2,1)} %param.5, f32[1024,192]{1,0:T(8,128)S(1)} %all_gather.6, f32[128]{0:T(128)S(1)} %multiply_reduce_fusion), kind=kOutput, calls=%fused_computation.15 | convolution fusion | flops 1076359168 | bytes 10781184 | tf_op jit(solution)/shard_map/dot_general | solution.py:88
  162.2 14.1 %all_to_all.59 = f32[16,1,4096]{2,1,0:T(1,128)S(1)} all-to-all(f32[16,1,4096]{2,1,0:T(1,128)S(1)} %broadcast_in_dim.47), channel_id=1, replica_groups=mesh['pts'=32,'cen'=16] {'cen'}, dimensions={0} | all-to-all | bytes 524288 | tf_op jit(solution)/shard_map/all_to_all | solution.py:14
  176.3 0.9 broadcast_in_dim.42
  177.2 3.5 %all-to-all-start.4 = ((f32[16,1,4096]{2,1,0:T(1,128)}), f32[16,1,4096]{2,1,0:T(1,128)S(1)}, u32[]{:S(2)}, u32[]{:S(2)}) async-start(f32[16,1,4096]{2,1,0:T(1,128)} %broadcast_in_dim.42), calls=%async_computation.4 | async-start | bytes 524288 | tf_op jit(solution)/shard_map/all_to_all | solution.py:14
  180.9 11.1 %all-to-all-done.4 = f32[16,1,4096]{2,1,0:T(1,128)S(1)} async-done(((f32[16,1,4096]{2,1,0:T(1,128)}), f32[16,1,4096]{2,1,0:T(1,128)S(1)}, u32[]{:S(2)}, u32[]{:S(2)}) %all-to-all-start.4) | async-done | bytes 262176 | tf_op jit(solution)/shard_map/all_to_all | solution.py:14
  193.2 6.6 %all-to-all-start.6 = ((f32[32,1,128]{2,1,0:T(1,128)}), f32[32,1,128]{2,1,0:T(1,128)S(1)}, u32[]{:S(2)}, u32[]{:S(2)}) async-start(f32[32,1,128]{2,1,0:T(1,128)} %broadcast_in_dim.44), calls=%async_computation.6 | async-start | bytes 32768 | tf_op jit(solution)/shard_map/all_to_all | solution.py:14
  199.9 8.1 %fusion.3 = f32[128,1024]{0,1:T(8,128)} fusion(bf16[4096,1024]{1,0:T(8,128)(2,1)} %param.5, f32[4096]{0:T(1024)S(1)} %get-tuple-element.22, s32[4096]{0:T(1024)S(1)} %bitcast.37), kind=kOutput, calls=%fused_computation.6 | convolution fusion | flops 1086849024 | bytes 8945664 | tf_op jit(solution)/shard_map/dot_general | solution.py:99
  208.3 9.4 %all-to-all-start.5 = ((f32[32,128,32]{1,2,0:T(8,128)}), f32[32,128,32]{1,2,0:T(8,128)S(1)}, u32[]{:S(2)}, u32[]{:S(2)}) async-start(f32[32,128,32]{1,2,0:T(8,128)} %bitcast.9), calls=%async_computation.5 | async-start | bytes 1048576 | tf_op jit(solution)/shard_map/all_to_all | solution.py:34
  217.9 16.8 %all-to-all-done.5 = f32[32,128,32]{1,2,0:T(8,128)S(1)} async-done(((f32[32,128,32]{1,2,0:T(8,128)}), f32[32,128,32]{1,2,0:T(8,128)S(1)}, u32[]{:S(2)}, u32[]{:S(2)}) %all-to-all-start.5) | async-done | bytes 524320 | tf_op jit(solution)/shard_map/all_to_all | solution.py:34
  235.2 0.7 broadcast_in_dim.45
  235.9 3.5 %all-to-all-start.7 = ((f32[16,1,2112]{2,1,0:T(1,128)}), f32[16,1,2112]{2,1,0:T(1,128)S(1)}, u32[]{:S(2)}, u32[]{:S(2)}) async-start(f32[16,1,2112]{2,1,0:T(1,128)} %broadcast_in_dim.45), calls=%async_computation.7 | async-start | bytes 278528 | tf_op jit(solution)/shard_map/all_to_all | solution.py:14
  239.4 0.6 pad_maximum_fusion.2
  240.1 8.1 %all-to-all-done.7 = f32[16,1,2112]{2,1,0:T(1,128)S(1)} async-done(((f32[16,1,2112]{2,1,0:T(1,128)}), f32[16,1,2112]{2,1,0:T(1,128)S(1)}, u32[]{:S(2)}, u32[]{:S(2)}) %all-to-all-start.7) | async-done | bytes 135200 | tf_op jit(solution)/shard_map/all_to_all | solution.py:14
  248.5 48.3 %all_gather.7 = f32[1024,192]{1,0:T(8,128)S(1)} all-gather(f32[32,192]{1,0:T(8,128)S(1)} %pad_maximum_fusion.1), channel_id=1, replica_groups=mesh['pts'=32,'cen'=16] {'pts'}, dimensions={0}, use_global_device_ids=true | all-gather | bytes 811008 | tf_op jit(solution)/shard_map/all_gather | solution.py:50
  296.9 1.0 copy.44
  297.9 0.9 copy.45
  (55 shorter events, 6.0 us)
Async XLA Ops:
  0.6 75.3 %copy-start = (f32[64,1024]{1,0:T(8,128)S(1)}, f32[64,1024]{1,0:T(8,128)}, u32[]{:S(2)}) copy-start(f32[64,1024]{1,0:T(8,128)} %param.8) | copy-start | bytes 786436
  31.7 14.9 %all-to-all-start = ((f32[16,1,4096]{2,1,0:T(1,128)}), f32[16,1,4096]{2,1,0:T(1,128)S(1)}, u32[]{:S(2)}, u32[]{:S(2)}) async-start(f32[16,1,4096]{2,1,0:T(1,128)} %broadcast_in_dim.38), calls=%async_computation | async-start | bytes 524288 | tf_op jit(solution)/shard_map/all_to_all | solution.py:14
  47.7 18.7 %all-to-all-start.2 = ((f32[32,1,128]{2,1,0:T(1,128)}), f32[32,1,128]{2,1,0:T(1,128)S(1)}, u32[]{:S(2)}, u32[]{:S(2)}) async-start(f32[32,1,128]{2,1,0:T(1,128)} %broadcast_in_dim.40), calls=%async_computation.2 | async-start | bytes 32768 | tf_op jit(solution)/shard_map/all_to_all | solution.py:14
  58.0 18.0 %copy-start.1 = (s32[128]{0:T(128)S(1)}, s32[128]{0:T(128)}, u32[]{:S(2)}) copy-start(s32[128]{0:T(128)} %param.9) | copy-start | bytes 1540
  66.5 26.4 %all-to-all-start.1 = ((f32[32,128,32]{1,2,0:T(8,128)}), f32[32,128,32]{1,2,0:T(8,128)S(1)}, u32[]{:S(2)}, u32[]{:S(2)}) async-start(f32[32,128,32]{1,2,0:T(8,128)} %bitcast.3), calls=%async_computation.1 | async-start | bytes 1048576 | tf_op jit(solution)/shard_map/all_to_all | solution.py:34
  94.1 12.3 %all-to-all-start.3 = ((f32[16,1,2112]{2,1,0:T(1,128)}), f32[16,1,2112]{2,1,0:T(1,128)S(1)}, u32[]{:S(2)}, u32[]{:S(2)}) async-start(f32[16,1,2112]{2,1,0:T(1,128)} %broadcast_in_dim.41), calls=%async_computation.3 | async-start | bytes 278528 | tf_op jit(solution)/shard_map/all_to_all | solution.py:14
  177.2 14.9 %all-to-all-start.4 = ((f32[16,1,4096]{2,1,0:T(1,128)}), f32[16,1,4096]{2,1,0:T(1,128)S(1)}, u32[]{:S(2)}, u32[]{:S(2)}) async-start(f32[16,1,4096]{2,1,0:T(1,128)} %broadcast_in_dim.42), calls=%async_computation.4 | async-start | bytes 524288 | tf_op jit(solution)/shard_map/all_to_all | solution.py:14
  193.2 15.1 %all-to-all-start.6 = ((f32[32,1,128]{2,1,0:T(1,128)}), f32[32,1,128]{2,1,0:T(1,128)S(1)}, u32[]{:S(2)}, u32[]{:S(2)}) async-start(f32[32,1,128]{2,1,0:T(1,128)} %broadcast_in_dim.44), calls=%async_computation.6 | async-start | bytes 32768 | tf_op jit(solution)/shard_map/all_to_all | solution.py:14
  208.3 26.4 %all-to-all-start.5 = ((f32[32,128,32]{1,2,0:T(8,128)}), f32[32,128,32]{1,2,0:T(8,128)S(1)}, u32[]{:S(2)}, u32[]{:S(2)}) async-start(f32[32,128,32]{1,2,0:T(8,128)} %bitcast.9), calls=%async_computation.5 | async-start | bytes 1048576 | tf_op jit(solution)/shard_map/all_to_all | solution.py:34
  235.9 12.3 %all-to-all-start.7 = ((f32[16,1,2112]{2,1,0:T(1,128)}), f32[16,1,2112]{2,1,0:T(1,128)S(1)}, u32[]{:S(2)}, u32[]{:S(2)}) async-start(f32[16,1,2112]{2,1,0:T(1,128)} %broadcast_in_dim.45), calls=%async_computation.7 | async-start | bytes 278528 | tf_op jit(solution)/shard_map/all_to_all | solution.py:14
where the time goes:
time: 300 us; the launch traced here: 299 us
  blocking collectives  132 us (44%)
  waiting for transfers between devices  68.4 us (23%)
  starting transfers between devices  49.8 us (17%)
  matrix products  29.8 us (10%)
  other arithmetic  10.1 us (3%)
  local copies, waits for them, and re-layouts  7.5 us (2%)
    all_gather x2, blocking collectives, rows_first(): filled = lax.all_gather(both, axis, axis=0, tiled=True)  96.8 us
    all_to_all x2, blocking collectives, copy_for_each(): lax.all_to_all(jnp.broadcast_to(x[None], (size, *x.shape)), axis, 0, 0, t...  35.5 us
    all_to_all x6, waiting for transfers between devices, copy_for_each(): lax.all_to_all(jnp.broadcast_to(x[None], (size, *x.shape)), axis, 0, 0, t...  34.8 us
    all_to_all x2, waiting for transfers between devices, sum_at_owner(): lax.all_to_all(blocks, axis, split_axis=0, concat_axis=0, tiled=True)  33.6 us
    all_to_all x6, starting transfers between devices, copy_for_each(): lax.all_to_all(jnp.broadcast_to(x[None], (size, *x.shape)), axis, 0, 0, t...  31 us
    all_to_all x2, starting transfers between devices, sum_at_owner(): lax.all_to_all(blocks, axis, split_axis=0, concat_axis=0, tiled=True)  18.8 us
    dot_general x2, matrix products, on_device(): lax.dot_general(member.astype(jnp.bfloat16), scaled, (((0,), (0,)), ((),...  16.2 us
    dot_general x2, matrix products, on_device(): jnp.dot(points, fine_now.astype(jnp.bfloat16).T, preferred_element_type=j...  13 us
  transfers between devices with their start and end apart: 8, of which 8 were waited for; matrix products, arithmetic and copies ran while one was open for 8% of the time, Pallas kernels for 0%

commit v1 on v0

--- a/solution.py
+++ b/solution.py
@@ -7,6 +7,11 @@
 NC = 64
 PASSES = 2
 prior_weight = 4.0
+
+
+def exchange_gather(x, axis, dim):
+    repeated = jnp.stack([x] * lax.axis_size(axis))
+    return jnp.concatenate(lax.all_to_all(repeated, axis, 0, 0), axis=dim)
 
 
 def copy_for_each(x, axis):
@@ -47,7 +52,7 @@
     turned = [jnp.moveaxis(a, dim, 0) for a, dim in zip(arrays, dims)]
     widths = [t[0].size for t in turned]
     both = jnp.concatenate([t.reshape(-1, w) for t, w in zip(turned, widths)], axis=1)
-    filled = lax.all_gather(both, axis, axis=0, tiled=True)
+    filled = exchange_gather(both, axis, 0)
     blocks = jnp.split(filled, [sum(widths[:k]) for k in range(1, len(widths))], axis=1)
     return tuple(
         (

time: 300 us -> 270 us (0.900)
  blocking collectives: 132 us -> 80.8 us
  waiting for transfers between devices: 68.4 us -> 88.4 us
    all_gather x2 -> x0, blocking collectives: 96.8 us -> none  [rows_first(): filled = lax.all_gather(both, axis, axis=0, tiled=True)]
    all_to_all x0 -> x1, blocking collectives: none -> 34.5 us  [exchange_gather(): return jnp.concatenate(lax.all_to_all(repeated, axis, 0, 0), axis=dim)]
    all_to_all x0 -> x1, waiting for transfers between devices: none -> 28.2 us  [exchange_gather(): return jnp.concatenate(lax.all_to_all(repeated, axis, 0, 0), axis=dim)]
    all_to_all x2 -> x3, blocking collectives: 35.5 us -> 46.3 us  [copy_for_each(): lax.all_to_all(jnp.broadcast_to(x[None], (size, *x.shape)), axis, 0, 0, t...]
    all_to_all x6 -> x5, waiting for transfers between devices: 34.8 us -> 26.7 us  [copy_for_each(): lax.all_to_all(jnp.broadcast_to(x[None], (size, *x.shape)), axis, 0, 0, t...]
    all_to_all x0 -> x1, starting transfers between devices: none -> 5.57 us  [exchange_gather(): return jnp.concatenate(lax.all_to_all(repeated, axis, 0, 0), axis=dim)]
    all_to_all x6 -> x5, starting transfers between devices: 31 us -> 26.4 us  [copy_for_each(): lax.all_to_all(jnp.broadcast_to(x[None], (size, *x.shape)), axis, 0, 0, t...]
where the time goes in v1:
time: 270 us; the launch traced here: 269 us
  waiting for transfers between devices  88.4 us (33%)
  blocking collectives  80.8 us (30%)
  starting transfers between devices  50.8 us (19%)
  matrix products  29.8 us (11%)
  other arithmetic  10.1 us (4%)
  local copies, waits for them, and re-layouts  8.06 us (3%)
    all_to_all x3, blocking collectives, copy_for_each(): lax.all_to_all(jnp.broadcast_to(x[None], (size, *x.shape)), axis, 0, 0, t...  46.3 us
    all_to_all x1, blocking collectives, exchange_gather(): return jnp.concatenate(lax.all_to_all(repeated, axis, 0, 0), axis=dim)  34.5 us
    all_to_all x2, waiting for transfers between devices, sum_at_owner(): lax.all_to_all(blocks, axis, split_axis=0, concat_axis=0, tiled=True)  33.6 us
    all_to_all x1, waiting for transfers between devices, exchange_gather(): return jnp.concatenate(lax.all_to_all(repeated, axis, 0, 0), axis=dim)  28.2 us
    all_to_all x5, waiting for transfers between devices, copy_for_each(): lax.all_to_all(jnp.broadcast_to(x[None], (size, *x.shape)), axis, 0, 0, t...  26.7 us
    all_to_all x5, starting transfers between devices, copy_for_each(): lax.all_to_all(jnp.broadcast_to(x[None], (size, *x.shape)), axis, 0, 0, t...  26.4 us
    all_to_all x2, starting transfers between devices, sum_at_owner(): lax.all_to_all(blocks, axis, split_axis=0, concat_axis=0, tiled=True)  18.8 us
    dot_general x2, matrix products, on_device(): lax.dot_general(member.astype(jnp.bfloat16), scaled, (((0,), (0,)), ((),...  16.2 us
  transfers between devices with their start and end apart: 8, of which 8 were waited for; matrix products, arithmetic and copies ran while one was open for 8% of the time, Pallas kernels for 0%

profile of v1, /device:TPU:2, one launch (start us, length us, event | category | flops | bytes accessed | tf_op | source)
XLA Modules:
  0.0 269.0 jit_solution(14290968520032491625)
XLA Ops:
  0.6 1.2 multiply_reduce_fusion.1
  1.9 0.9 slice_subtract_fusion.1
  2.7 6.5 %fusion.33 = (f32[4096]{0:T(1024)S(1)}, f32[4096]{0:T(1024)S(1)}) fusion(s32[4096]{0:T(1024)S(1)} %bitcast.51, bf16[4096,1024]{1,0:T(8,128)(2,1)} %param.5, f32[128,1024]{1,0:T(8,128)} %param.7, f32[128]{0:T(128)S(1)} %multiply_reduce_fusion.1), kind=kOutput, calls=%fused_computation.70 | convolution fusion | flops 1077010432 | bytes 8962560 | tf_op jit(solution)/shard_map/dot_general | solution.py:93
  9.4 21.4 %all_to_all.68 = f32[16,1,4096]{2,1,0:T(1,128)S(1)} all-to-all(f32[16,1,4096]{2,1,0:T(1,128)S(1)} %broadcast_in_dim.46), channel_id=1, replica_groups=mesh['pts'=32,'cen'=16] {'cen'}, dimensions={0} | all-to-all | bytes 524288 | tf_op jit(solution)/shard_map/all_to_all | solution.py:19
  30.8 0.9 broadcast_in_dim.38
  31.7 3.5 %all-to-all-start = ((f32[16,1,4096]{2,1,0:T(1,128)}), f32[16,1,4096]{2,1,0:T(1,128)S(1)}, u32[]{:S(2)}, u32[]{:S(2)}) async-start(f32[16,1,4096]{2,1,0:T(1,128)} %broadcast_in_dim.38), calls=%async_computation | async-start | bytes 524288 | tf_op jit(solution)/shard_map/all_to_all | solution.py:19
  35.2 5.1 %fusion = f32[4096]{0:T(1024)S(1)} fusion(bf16[4096,1024]{1,0:T(8,128)(2,1)} %param.5), kind=kLoop, calls=%fused_computation.3 | loop fusion | flops 12578816 | bytes 8404992 | tf_op jit(solution)/shard_map/reduce_sum | solution.py:87
  40.5 6.0 %all-to-all-done = f32[16,1,4096]{2,1,0:T(1,128)S(1)} async-done(((f32[16,1,4096]{2,1,0:T(1,128)}), f32[16,1,4096]{2,1,0:T(1,128)S(1)}, u32[]{:S(2)}, u32[]{:S(2)}) %all-to-all-start) | async-done | bytes 262176 | tf_op jit(solution)/shard_map/all_to_all | solution.py:19
  47.7 10.2 %all-to-all-start.2 = ((f32[32,1,128]{2,1,0:T(1,128)}), f32[32,1,128]{2,1,0:T(1,128)S(1)}, u32[]{:S(2)}, u32[]{:S(2)}) async-start(f32[32,1,128]{2,1,0:T(1,128)} %broadcast_in_dim.40), calls=%async_computation.2 | async-start | bytes 32768 | tf_op jit(solution)/shard_map/all_to_all | solution.py:19
  58.0 8.1 %fusion.5 = f32[128,1024]{0,1:T(8,128)} fusion(bf16[4096,1024]{1,0:T(8,128)(2,1)} %param.5, f32[4096]{0:T(1024)S(1)} %get-tuple-element.17, s32[4096]{0:T(1024)S(1)} %bitcast.53), kind=kOutput, calls=%fused_computation.7 | convolution fusion | flops 1086849024 | bytes 8945664 | tf_op jit(solution)/shard_map/dot_general | solution.py:104
  66.5 9.4 %all-to-all-start.1 = ((f32[32,128,32]{1,2,0:T(8,128)}), f32[32,128,32]{1,2,0:T(8,128)S(1)}, u32[]{:S(2)}, u32[]{:S(2)}) async-start(f32[32,128,32]{1,2,0:T(8,128)} %bitcast.3), calls=%async_computation.1 | async-start | bytes 1048576 | tf_op jit(solution)/shard_map/all_to_all | solution.py:39
  76.1 16.8 %all-to-all-done.1 = f32[32,128,32]{1,2,0:T(8,128)S(1)} async-done(((f32[32,128,32]{1,2,0:T(8,128)}), f32[32,128,32]{1,2,0:T(8,128)S(1)}, u32[]{:S(2)}, u32[]{:S(2)}) %all-to-all-start.1) | async-done | bytes 524320 | tf_op jit(solution)/shard_map/all_to_all | solution.py:39
  93.4 0.7 broadcast_in_dim.41
  94.1 3.5 %all-to-all-start.3 = ((f32[16,1,2112]{2,1,0:T(1,128)}), f32[16,1,2112]{2,1,0:T(1,128)S(1)}, u32[]{:S(2)}, u32[]{:S(2)}) async-start(f32[16,1,2112]{2,1,0:T(1,128)} %broadcast_in_dim.41), calls=%async_computation.3 | async-start | bytes 278528 | tf_op jit(solution)/shard_map/all_to_all | solution.py:19
  97.7 8.7 %all-to-all-done.3 = f32[16,1,2112]{2,1,0:T(1,128)S(1)} async-done(((f32[16,1,2112]{2,1,0:T(1,128)}), f32[16,1,2112]{2,1,0:T(1,128)S(1)}, u32[]{:S(2)}, u32[]{:S(2)}) %all-to-all-start.3) | async-done | bytes 135200 | tf_op jit(solution)/shard_map/all_to_all | solution.py:19
  106.8 34.5 %all_to_all.69 = f32[32,32,192]{2,1,0:T(8,128)S(1)} all-to-all(f32[32,32,192]{2,1,0:T(8,128)S(1)} %stack.6), channel_id=1, replica_groups=mesh['pts'=32,'cen'=16] {'pts'}, dimensions={0} | all-to-all | bytes 1572864 | tf_op jit(solution)/shard_map/all_to_all | solution.py:14
  141.5 6.5 %fusion.11 = (f32[4096]{0:T(1024)S(1)}, f32[128,4096]{1,0:T(8,128)S(1)}) fusion(s32[4096]{0:T(1024)S(1)} %bitcast.42, bf16[4096,1024]{1,0:T(8,128)(2,1)} %param.5, f32[1024,192]{1,0:T(8,128)S(1)} %bitcast.38, f32[128]{0:T(128)S(1)} %multiply_reduce_fusion), kind=kOutput, calls=%fused_computation.15 | convolution fusion | flops 1076359168 | bytes 10781184 | tf_op jit(solution)/shard_map/dot_general | solution.py:93
  148.3 13.6 %all_to_all.70 = f32[16,1,4096]{2,1,0:T(1,128)S(1)} all-to-all(f32[16,1,4096]{2,1,0:T(1,128)S(1)} %broadcast_in_dim.47), channel_id=1, replica_groups=mesh['pts'=32,'cen'=16] {'cen'}, dimensions={0} | all-to-all | bytes 524288 | tf_op jit(solution)/shard_map/all_to_all | solution.py:19
  161.9 0.9 broadcast_in_dim.42
  162.8 3.5 %all-to-all-start.5 = ((f32[16,1,4096]{2,1,0:T(1,128)}), f32[16,1,4096]{2,1,0:T(1,128)S(1)}, u32[]{:S(2)}, u32[]{:S(2)}) async-start(f32[16,1,4096]{2,1,0:T(1,128)} %broadcast_in_dim.42), calls=%async_computation.5 | async-start | bytes 524288 | tf_op jit(solution)/shard_map/all_to_all | solution.py:19
  166.5 11.2 %all-to-all-done.5 = f32[16,1,4096]{2,1,0:T(1,128)S(1)} async-done(((f32[16,1,4096]{2,1,0:T(1,128)}), f32[16,1,4096]{2,1,0:T(1,128)S(1)}, u32[]{:S(2)}, u32[]{:S(2)}) %all-to-all-start.5) | async-done | bytes 262176 | tf_op jit(solution)/shard_map/all_to_all | solution.py:19
  178.9 5.6 %all-to-all-start.7 = ((f32[32,1,128]{2,1,0:T(1,128)}), f32[32,1,128]{2,1,0:T(1,128)S(1)}, u32[]{:S(2)}, u32[]{:S(2)}) async-start(f32[32,1,128]{2,1,0:T(1,128)} %broadcast_in_dim.44), calls=%async_computation.7 | async-start | bytes 32768 | tf_op jit(solution)/shard_map/all_to_all | solution.py:19
  184.4 8.1 %fusion.3 = f32[128,1024]{0,1:T(8,128)} fusion(bf16[4096,1024]{1,0:T(8,128)(2,1)} %param.5, f32[4096]{0:T(1024)S(1)} %get-tuple-element.19, s32[4096]{0:T(1024)S(1)} %bitcast.44), kind=kOutput, calls=%fused_computation.6 | convolution fusion | flops 1086849024 | bytes 8945664 | tf_op jit(solution)/shard_map/dot_general | solution.py:104
  192.9 9.4 %all-to-all-start.6 = ((f32[32,128,32]{1,2,0:T(8,128)}), f32[32,128,32]{1,2,0:T(8,128)S(1)}, u32[]{:S(2)}, u32[]{:S(2)}) async-start(f32[32,128,32]{1,2,0:T(8,128)} %bitcast.10), calls=%async_computation.6 | async-start | bytes 1048576 | tf_op jit(solution)/shard_map/all_to_all | solution.py:39
  202.5 16.8 %all-to-all-done.6 = f32[32,128,32]{1,2,0:T(8,128)S(1)} async-done(((f32[32,128,32]{1,2,0:T(8,128)}), f32[32,128,32]{1,2,0:T(8,128)S(1)}, u32[]{:S(2)}, u32[]{:S(2)}) %all-to-all-start.6) | async-done | bytes 524320 | tf_op jit(solution)/shard_map/all_to_all | solution.py:39
  219.8 11.4 %all_to_all.71 = f32[16,1,2112]{2,1,0:T(1,128)S(1)} all-to-all(f32[16,1,2112]{2,1,0:T(1,128)S(1)} %broadcast_in_dim.45), channel_id=1, replica_groups=mesh['pts'=32,'cen'=16] {'cen'}, dimensions={0} | all-to-all | bytes 270336 | tf_op jit(solution)/shard_map/all_to_all | solution.py:19
  231.5 1.1 stack.7
  232.6 5.6 %all-to-all-start.9 = ((f32[32,32,192]{2,1,0:T(8,128)}), f32[32,32,192]{2,1,0:T(8,128)S(1)}, u32[]{:S(2)}, u32[]{:S(2)}) async-start(f32[32,32,192]{2,1,0:T(8,128)} %stack.7), calls=%async_computation.9 | async-start | bytes 2097152 | tf_op jit(solution)/shard_map/all_to_all | solution.py:14
  238.2 0.6 pad_maximum_fusion.2
  238.8 28.2 %all-to-all-done.9 = f32[32,32,192]{2,1,0:T(8,128)S(1)} async-done(((f32[32,32,192]{2,1,0:T(8,128)}), f32[32,32,192]{2,1,0:T(8,128)S(1)}, u32[]{:S(2)}, u32[]{:S(2)}) %all-to-all-start.9) | async-done | bytes 786464 | tf_op jit(solution)/shard_map/all_to_all | solution.py:14
  267.1 1.0 copy.43
  268.1 0.9 copy.44
  (57 shorter events, 6.2 us)
Async XLA Ops:
  0.6 75.3 %copy-start = (f32[64,1024]{1,0:T(8,128)S(1)}, f32[64,1024]{1,0:T(8,128)}, u32[]{:S(2)}) copy-start(f32[64,1024]{1,0:T(8,128)} %param.8) | copy-start | bytes 786436
  31.7 14.9 %all-to-all-start = ((f32[16,1,4096]{2,1,0:T(1,128)}), f32[16,1,4096]{2,1,0:T(1,128)S(1)}, u32[]{:S(2)}, u32[]{:S(2)}) async-start(f32[16,1,4096]{2,1,0:T(1,128)} %broadcast_in_dim.38), calls=%async_computation | async-start | bytes 524288 | tf_op jit(solution)/shard_map/all_to_all | solution.py:19
  47.7 18.7 %all-to-all-start.2 = ((f32[32,1,128]{2,1,0:T(1,128)}), f32[32,1,128]{2,1,0:T(1,128)S(1)}, u32[]{:S(2)}, u32[]{:S(2)}) async-start(f32[32,1,128]{2,1,0:T(1,128)} %broadcast_in_dim.40), calls=%async_computation.2 | async-start | bytes 32768 | tf_op jit(solution)/shard_map/all_to_all | solution.py:19
  58.0 18.0 %copy-start.1 = (s32[128]{0:T(128)S(1)}, s32[128]{0:T(128)}, u32[]{:S(2)}) copy-start(s32[128]{0:T(128)} %param.9) | copy-start | bytes 1540
  66.5 26.4 %all-to-all-start.1 = ((f32[32,128,32]{1,2,0:T(8,128)}), f32[32,128,32]{1,2,0:T(8,128)S(1)}, u32[]{:S(2)}, u32[]{:S(2)}) async-start(f32[32,128,32]{1,2,0:T(8,128)} %bitcast.3), calls=%async_computation.1 | async-start | bytes 1048576 | tf_op jit(solution)/shard_map/all_to_all | solution.py:39
  94.1 12.3 %all-to-all-start.3 = ((f32[16,1,2112]{2,1,0:T(1,128)}), f32[16,1,2112]{2,1,0:T(1,128)S(1)}, u32[]{:S(2)}, u32[]{:S(2)}) async-start(f32[16,1,2112]{2,1,0:T(1,128)} %broadcast_in_dim.41), calls=%async_computation.3 | async-start | bytes 278528 | tf_op jit(solution)/shard_map/all_to_all | solution.py:19
  162.8 14.9 %all-to-all-start.5 = ((f32[16,1,4096]{2,1,0:T(1,128)}), f32[16,1,4096]{2,1,0:T(1,128)S(1)}, u32[]{:S(2)}, u32[]{:S(2)}) async-start(f32[16,1,4096]{2,1,0:T(1,128)} %broadcast_in_dim.42), calls=%async_computation.5 | async-start | bytes 524288 | tf_op jit(solution)/shard_map/all_to_all | solution.py:19
  178.9 14.1 %all-to-all-start.7 = ((f32[32,1,128]{2,1,0:T(1,128)}), f32[32,1,128]{2,1,0:T(1,128)S(1)}, u32[]{:S(2)}, u32[]{:S(2)}) async-start(f32[32,1,128]{2,1,0:T(1,128)} %broadcast_in_dim.44), calls=%async_computation.7 | async-start | bytes 32768 | tf_op jit(solution)/shard_map/all_to_all | solution.py:19
  192.9 26.4 %all-to-all-start.6 = ((f32[32,128,32]{1,2,0:T(8,128)}), f32[32,128,32]{1,2,0:T(8,128)S(1)}, u32[]{:S(2)}, u32[]{:S(2)}) async-start(f32[32,128,32]{1,2,0:T(8,128)} %bitcast.10), calls=%async_computation.6 | async-start | bytes 1048576 | tf_op jit(solution)/shard_map/all_to_all | solution.py:39
  232.6 34.4 %all-to-all-start.9 = ((f32[32,32,192]{2,1,0:T(8,128)}), f32[32,32,192]{2,1,0:T(8,128)S(1)}, u32[]{:S(2)}, u32[]{:S(2)}) async-start(f32[32,32,192]{2,1,0:T(8,128)} %stack.7), calls=%async_computation.9 | async-start | bytes 2097152 | tf_op jit(solution)/shard_map/all_to_all | solution.py:14
